TPU v7x, 32 devices: a whole 2x2x4 slice. The times are simulated.
32 devices in a mesh: pb: 4 (over x, core), pq: 8 (over z, y).
Axes of the slice: x: 2, y: 2, z: 4, core: 2. Of those that a mesh axis runs over, the one named last changes fastest.
Arguments:
- chol_vv: bfloat16 [176, 1792, 1792], P('pb', 'pq'), may hold values from -6 to 6
- chol_ov: bfloat16 [176, 256, 1792], P('pb', 'pq'), may hold values from -6 to 6
- chol_oo: bfloat16 [176, 256, 256], P('pb', 'pq'), may hold values from -6 to 6
- chol_vo: bfloat16 [176, 256, 1792], P('pb', None, 'pq'), may hold values from -6 to 6
- amplitudes: bfloat16 [256, 1792], P(None, 'pq'), may hold values from -0.125 to 0.125
Outputs:
- dressed: bfloat16 [176, 256, 1792], P('pb', 'pq')
- fock_ov: float32 [256, 1792], P('pq')
All inputs are finite; a program needn't handle non-finite values.
Results may differ from a plain program's by a relative error of at most 0.0081.
Values may be sent and summed in bfloat16 or wider, within the bound.
A program may use at most 128 MiB of HBM per device.

v0:
```python
import jax
import jax.numpy as jnp
from jax import lax
from jax.sharding import PartitionSpec as P


def per_device(chol_vv, chol_ov, chol_oo, chol_vo, amplitudes):
    batch = chol_vv.shape[0]
    occ_rows = chol_ov.shape[1]
    whole_amps = lax.all_gather(amplitudes, "pq", axis=1, tiled=True)
    lprime = (
        chol_oo.astype(jnp.float32)
        + jnp.einsum("qjb,ib->qji", chol_ov, whole_amps, preferred_element_type=jnp.float32)
    ).astype(jnp.bfloat16)
    direct = jnp.einsum("qab,ib->qia", chol_vv, whole_amps, preferred_element_type=jnp.float32)
    partial_sum = chol_vo.astype(jnp.float32) + direct
    occupied = jnp.einsum(
        "qji,ja->qia",
        lax.all_gather(lprime, "pq", axis=1, tiled=True),
        amplitudes,
        preferred_element_type=jnp.float32,
    )
    local_dressed = (partial_sum - occupied).astype(jnp.bfloat16)
    dressed = lax.all_to_all(local_dressed, "pq", split_axis=1, concat_axis=2, tiled=True)
    row_start = lax.axis_index("pq") * occ_rows
    own_amps = lax.dynamic_slice_in_dim(whole_amps, row_start, occ_rows, 0)
    local_coulomb = 2.0 * jnp.einsum(
        "qia,ia->q", dressed, own_amps, preferred_element_type=jnp.float32
    )
    coulomb = lax.psum(local_coulomb, "pq")
    local_fock = jnp.sum(coulomb[:, None, None] * dressed.astype(jnp.float32), axis=0)
    fock_ov = lax.psum(local_fock, "pb") / (batch * lax.axis_size("pb"))
    return (dressed, fock_ov)


def solution(mesh):
    in_specs = (
        P("pb", "pq", None),
        P("pb", "pq", None),
        P("pb", "pq", None),
        P("pb", None, "pq"),
        P(None, "pq"),
    )
    out_specs = (P("pb", "pq", None), P("pq", None))
    return jax.shard_map(
        per_device, mesh=mesh, in_specs=in_specs, out_specs=out_specs, check_vma=False
    )
```

profile of v0, /device:TPU:0, one launch (start us, length us, event | category | flops | bytes accessed | tf_op | source)
XLA Modules:
  0.0 394.0 jit_solution(11344486963419450905)
XLA Ops:
  7.2 0.0 all-gather.2.cloned.1.call-start
  7.2 34.5 %all_gather.6 = bf16[256,1792]{0,1:T(8,128)(2,1)S(1)} all-gather(bf16[256,224]{0,1:T(8,128)(2,1)} %param.9), channel_id=1, replica_groups=mesh['pb'=4,'pq'=8] {'pq'}, dimensions={1}, use_global_device_ids=true | all-gather | bytes 1032192 | tf_op jit(solution)/shard_map/all_gather | solution.py:10
  41.7 5.0 %add_convert_fusion = bf16[44,32,256]{2,1,0:T(8,128)(2,1)} fusion(bf16[44,32,256]{2,1,0:T(8,128)(2,1)} %param.7, bf16[44,32,1792]{2,1,0:T(8,128)(2,1)} %param.6, bf16[256,1792]{0,1:T(8,128)(2,1)S(1)} %all_gather.6), kind=kOutput, calls=%fused_computation.6 | convolution fusion | flops 1292926976 | bytes 7405568 | tf_op jit(solution)/shard_map/qjb,ib->qji/dot_general | solution.py:13
  46.6 0.0 all-gather.2.cloned.1.call-update
  46.6 0.0 copy-start
  46.7 19.8 %fusion.11 = f32[256,44,224]{0,2,1:T(8,128)} fusion(bf16[44,224,1792]{2,1,0:T(8,128)(2,1)} %param.5, bf16[256,1792]{0,1:T(8,128)(2,1)S(1)} %all_gather.6), kind=kOutput, calls=%fused_computation.10 | convolution fusion | flops 9042919424 | bytes 46333952 | tf_op jit(solution)/shard_map/qab,ib->qia/dot_general | solution.py:15
  66.4 73.5 %all-gather.2.cloned.1.call-done = bf16[44,256,256]{2,1,0:T(8,128)(2,1)} async-done(((bf16[44,32,256]{2,1,0:T(8,128)(2,1)}), bf16[44,256,256]{2,1,0:T(8,128)(2,1)}) %all-gather.2.cloned.1.call-update) | async-done | bytes 5767184 | tf_op jit(solution)/shard_map/all_gather | solution.py:19
  139.9 0.0 copy-done
  139.9 10.7 %fusion.1 = bf16[44,256,224]{1,2,0:T(8,128)(2,1)} fusion(f32[256,44,224]{0,2,1:T(8,128)} %fusion.11, bf16[44,256,224]{1,2,0:T(8,128)(2,1)} %param.8, bf16[44,256,256]{2,1,0:T(8,128)(2,1)} %all-gather.2.cloned.1.call-done, bf16[256,224]{0,1:T(8,128)(2,1)S(1)} %copy-done), kind=kOutput, calls=%fused_computation.3 | convolution fusion | flops 1301938176 | bytes 26066944 | tf_op jit(solution)/shard_map/qji,ja->qia/dot_general | solution.py:17
  150.6 8.8 %copy.14 = bf16[44,256,224]{2,0,1:T(8,128)(2,1)} copy(bf16[44,256,224]{1,2,0:T(8,128)(2,1)} %fusion.1) | data formatting | bytes 10092544 | tf_op jit(solution)/shard_map/convert_element_type | solution.py:23
  159.5 4.7 %all-to-all-start = ((bf16[44,256,224]{2,0,1:T(8,128)(2,1)}), bf16[44,256,224]{2,0,1:T(8,128)(2,1)}, u32[]{:S(2)}, u32[]{:S(2)}) async-start(bf16[44,256,224]{2,0,1:T(8,128)(2,1)} %copy.14), calls=%async_computation | async-start | bytes 12582912 | tf_op jit(solution)/shard_map/all_to_all | solution.py:24
  164.2 0.2 all-reduce.2.cloned.1.call-start
  164.5 0.2 dynamic-slice_bitcast_fusion
  164.7 0.3 copy.19
  165.0 136.1 %all-to-all-done = bf16[44,256,224]{2,0,1:T(8,128)(2,1)} async-done(((bf16[44,256,224]{2,0,1:T(8,128)(2,1)}), bf16[44,256,224]{2,0,1:T(8,128)(2,1)}, u32[]{:S(2)}, u32[]{:S(2)}) %all-to-all-start) | async-done | bytes 5046304 | tf_op jit(solution)/shard_map/all_to_all | solution.py:24
  301.1 8.6 %copy.16 = bf16[44,32,8,224]{3,2,1,0:T(8,128)(2,1)} copy(bf16[44,32,8,224]{3,0,1,2:T(8,128)(2,1)} %bitcast.5) | data formatting | bytes 10092544 | tf_op jit(solution)/shard_map/all_to_all | solution.py:24
  309.7 11.0 %all_to_all.16 = bf16[44,32,1792]{2,1,0:T(8,128)(2,1)} reshape(bf16[44,32,8,224]{3,2,1,0:T(8,128)(2,1)} %copy.16) | data formatting | bytes 10092544 | tf_op jit(solution)/shard_map/all_to_all | solution.py:24
  320.7 7.9 %fusion.7 = f32[44]{0:T(128)S(1)} fusion(bf16[32,1792,1]{1,2,0:T(2,128)(2,1)S(1)} %copy.19, bf16[44,32,1792]{2,1,0:T(8,128)(2,1)} %all_to_all.16), kind=kOutput, calls=%fused_computation.8 | convolution fusion | flops 5046316 | bytes 5161136 | tf_op jit(solution)/shard_map/qia,ia->q/dot_general | solution.py:27
  328.5 19.7 %psum.14 = f32[44]{0:T(128)S(1)} all-reduce(f32[44]{0:T(128)S(1)} %fusion.7), channel_id=1, replica_groups=mesh['pb'=4,'pq'=8] {'pq'}, use_global_device_ids=true, to_apply=%region_0.0 | all-reduce | flops 44 | bytes 352 | tf_op jit(solution)/shard_map/psum | solution.py:30
  348.2 4.8 %copy.15 = bf16[44,256,224]{2,1,0:T(8,128)(2,1)S(1)} copy(bf16[44,256,224]{2,0,1:T(8,128)(2,1)} %all-to-all-done) | data formatting | bytes 10092544 | tf_op jit(solution)/shard_map/all_to_all | solution.py:24
  353.0 1.9 multiply_reduce_fusion
  354.9 0.2 copy.17
  355.0 0.8 reduce_sum.12
  355.9 0.0 all-reduce.2.cloned.1.call-update
  355.9 29.6 %all-reduce.2.cloned.1.call-done = f32[32,1792]{1,0:T(8,128)} async-done(((f32[32,1792]{1,0:T(8,128)}), f32[32,1792]{1,0:T(8,128)}) %all-reduce.2.cloned.1.call-update) | async-done | bytes 229392 | tf_op jit(solution)/shard_map/psum | solution.py:32
  385.5 1.6 broadcast_multiply_fusion
Async XLA Ops:
  7.2 132.8 %all-gather.2.cloned.1.call-start = ((), (), s32[]{:S(2)}) async-start(), calls=%async_computation.1 | async-start | bytes 6488064 | tf_op jit(solution)/shard_map/all_gather | solution.py:19
  46.6 93.3 %copy-start = (bf16[256,224]{0,1:T(8,128)(2,1)S(1)}, bf16[256,224]{0,1:T(8,128)(2,1)}, u32[]{:S(2)}) copy-start(bf16[256,224]{0,1:T(8,128)(2,1)} %param.9) | copy-start | bytes 344068
  159.5 141.6 %all-to-all-start = ((bf16[44,256,224]{2,0,1:T(8,128)(2,1)}), bf16[44,256,224]{2,0,1:T(8,128)(2,1)}, u32[]{:S(2)}, u32[]{:S(2)}) async-start(bf16[44,256,224]{2,0,1:T(8,128)(2,1)} %copy.14), calls=%async_computation | async-start | bytes 12582912 | tf_op jit(solution)/shard_map/all_to_all | solution.py:24
  164.2 221.2 %all-reduce.2.cloned.1.call-start = ((), (), s32[]{:S(2)}) async-start(), calls=%async_computation.2 | async-start | bytes 458752 | tf_op jit(solution)/shard_map/psum | solution.py:32
Sparse Core Ops, SparseCore 0:
  46.8 93.1 all-gather.1
  356.0 29.4 all-reduce.1
where the time goes:
time: 395 us; the launch traced here: 394 us
  waiting for transfers between devices  239 us (61%)
  blocking collectives  54.1 us (14%)
  matrix products  43.3 us (11%)
  local copies, waits for them, and re-layouts  34.7 us (9%)
  between operations  14.1 us (4%)
  starting transfers between devices  5.01 us (1%)
    all_to_all x1, waiting for transfers between devices, per_device(): lax.all_to_all(local_dressed, 'pq', split_axis=1, concat_axis=2, tiled=True)  136 us
    all_gather x1, waiting for transfers between devices, per_device(): lax.all_gather(lprime, 'pq', axis=1, tiled=True)  73.5 us
    all_gather x1, blocking collectives, per_device(): whole_amps = lax.all_gather(amplitudes, 'pq', axis=1, tiled=True)  34.5 us
    psum x1, waiting for transfers between devices, per_device(): fock_ov = lax.psum(local_fock, 'pb') / (batch * lax.axis_size('pb'))  29.6 us
    all_to_all x3, local copies, waits for them, and re-layouts, per_device(): lax.all_to_all(local_dressed, 'pq', split_axis=1, concat_axis=2, tiled=True)  24.4 us
    dot_general x1, matrix products, per_device(): jnp.einsum('qab,ib->qia', chol_vv, whole_amps, preferred_element_type=jnp...  19.8 us
    psum x1, blocking collectives, per_device(): coulomb = lax.psum(local_coulomb, 'pq')  19.7 us
    dot_general x1, matrix products, per_device(): jnp.einsum('qji,ja->qia', lax.all_gather(lprime, 'pq', axis=1, tiled=True...  10.7 us
  transfers between devices with their start and end apart: 3, of which 3 were waited for; matrix products, arithmetic and copies ran while one was open for 5% of the time, Pallas kernels for 0%

commit v1 on v0

--- a/solution.py
+++ b/solution.py
@@ -1,7 +1,13 @@
+import functools
+
 import jax
 import jax.numpy as jnp
 from jax import lax
+from jax.experimental import pallas as pl
+from jax.experimental.pallas import tpu as pltpu
 from jax.sharding import PartitionSpec as P
+
+MESH = pl.DeviceIdType.MESH
 
 
 def per_device(chol_vv, chol_ov, chol_oo, chol_vo, amplitudes):
@@ -33,7 +39,246 @@
     return (dressed, fock_ov)
 
 
+def kernel(
+    n, n_pb, group,
+    vv_hbm, ov_hbm, oo_hbm, vo_hbm, amps_ref,
+    out_hbm, fock_ref,
+    vv_buf, ov_buf, oo_buf, vo_buf, amps_t, amps, tiled, gram,
+    sent, got, dressed, coul_sent, coul_got, fock_sent, fock_got,
+    load_sem, own_sem, gather_send, gather_recv, send_sem, recv_sem,
+    coul_send, coul_recv, fock_send, fock_recv, out_sem,
+):
+    me = lax.axis_index("pq")
+    mine = lax.axis_index("pb")
+    batch, virt, whole_virt = vv_hbm.shape
+    rows, occ = ov_hbm.shape[1], oo_hbm.shape[2]
+    steps = batch // group
+    wide, deep = group * virt, group * rows
+    peers = [lax.rem(me + d, n) for d in range(1, n)]
+    partners = [mine + 1 - 2 * lax.rem(mine, 2)] if n_pb >= 2 else []
+    if n_pb >= 4:
+        partners.append(lax.rem(mine + 2, 4))
+
+    def loads(step, slot):
+        part = pl.ds(step * group, group)
+        pairs = ((vv_hbm, vv_buf), (ov_hbm, ov_buf), (oo_hbm, oo_buf), (vo_hbm, vo_buf))
+        return [
+            pltpu.make_async_copy(src.at[part], dst.at[slot], load_sem.at[slot, k])
+            for k, (src, dst) in enumerate(pairs)
+        ]
+
+    for copy in loads(0, 0):
+        copy.start()
+
+    barrier = pltpu.get_barrier_semaphore()
+    for peer in peers:
+        pl.semaphore_signal(barrier, inc=1, device_id={"pq": peer}, device_id_type=MESH)
+    for partner in partners:
+        pl.semaphore_signal(barrier, inc=1, device_id={"pb": partner}, device_id_type=MESH)
+    pl.semaphore_wait(barrier, len(peers) + len(partners))
+
+    def remote(src, dst, send, recv, where):
+        return pltpu.make_async_remote_copy(
+            src_ref=src, dst_ref=dst, send_sem=send, recv_sem=recv,
+            device_id=where, device_id_type=MESH,
+        )
+
+    own_block = pl.ds(pl.multiple_of(me * virt, 16), virt)
+    gathers = [
+        remote(amps_ref, amps_t.at[own_block], gather_send.at[d], gather_recv.at[d], {"pq": peer})
+        for d, peer in enumerate(peers)
+    ]
+    for copy in gathers:
+        copy.start()
+    own = pltpu.make_async_copy(amps_ref, amps_t.at[own_block], own_sem)
+    own.start()
+    own.wait()
+    for copy in gathers:
+        copy.wait()
+
+    for s in range(n):
+        block = amps_t[s * virt:(s + 1) * virt, :]
+        amps_t_f32 = block.astype(jnp.float32)
+        tiled[:, s * virt:(s + 1) * virt] = amps_t_f32.T
+    for s in range(n):
+        part = tiled[s * rows:(s + 1) * rows, :].astype(jnp.bfloat16)
+        for q in range(group):
+            amps[s * deep + q * rows:s * deep + (q + 1) * rows, :] = part
+    own_rows = amps[pl.ds(pl.multiple_of(me * deep, 128), rows), :]
+    gram[...] = jnp.dot(own_rows, amps_t[...], preferred_element_type=jnp.float32)
+    coul_sent[...] = jnp.zeros_like(coul_sent)
+
+    def exchange(step, d):
+        return remote(
+            sent.at[step, pl.ds(pl.multiple_of(peers[d] * rows, 16), rows)],
+            got.at[step, me],
+            send_sem.at[step, d], recv_sem.at[step, d], {"pq": peers[d]},
+        )
+
+    def produce(step, carry):
+        slot = lax.rem(step, 2)
+
+        @pl.when(step + 1 < steps)
+        def _():
+            for copy in loads(step + 1, 1 - slot):
+                copy.start()
+
+        for copy in loads(step, slot):
+            copy.wait()
+        vv = vv_buf[slot].reshape(wide, whole_virt)
+        direct = jnp.dot(vv, amps_t[...], preferred_element_type=jnp.float32)
+        direct = direct + vo_buf[slot].reshape(wide, occ).astype(jnp.float32)
+        sent[step, :, 0:wide] = direct.T.astype(jnp.bfloat16)
+        ov = ov_buf[slot].reshape(deep, whole_virt)
+        lprime = jnp.dot(ov, amps_t[...], preferred_element_type=jnp.float32)
+        lprime = lprime + oo_buf[slot].reshape(deep, occ).astype(jnp.float32)
+        sent[step, :, wide:wide + deep] = lprime.T.astype(jnp.bfloat16)
+        own_amps = amps_ref[...].astype(jnp.float32)
+        at_row = lax.broadcasted_iota(jnp.int32, coul_sent.shape, 0) == step
+        lane = lax.broadcasted_iota(jnp.int32, coul_sent.shape, 1)
+        held = coul_sent[...]
+        for q in range(group):
+            from_direct = direct[q * virt:(q + 1) * virt] * own_amps
+            from_occ = lprime[q * rows:(q + 1) * rows] * gram[...]
+            value = jnp.sum(from_direct) - jnp.sum(from_occ)
+            held = jnp.where(at_row & (lane == q), value, held)
+        coul_sent[...] = held
+        got[step, me] = sent[step, pl.ds(pl.multiple_of(me * rows, 16), rows), :]
+        for d in range(n - 1):
+            exchange(step, d).start()
+        return carry
+
+    lax.fori_loop(0, steps, produce, 0)
+
+    coulombs = [
+        remote(coul_sent, coul_got.at[d], coul_send.at[d], coul_recv.at[d], {"pq": peer})
+        for d, peer in enumerate(peers)
+    ]
+    for copy in coulombs:
+        copy.start()
+
+    def out_copy(step):
+        part = pl.ds(step * group, group)
+        return pltpu.make_async_copy(dressed.at[part], out_hbm.at[part], out_sem.at[step])
+
+    def consume(step, carry):
+        for d in range(n - 1):
+            exchange(step, d).wait()
+        lane_q = lax.broadcasted_iota(jnp.int32, (rows, deep), 1) // rows
+        columns = []
+        for s in range(n):
+            piece = got[step, s, :, wide:wide + deep]
+            columns.append(jnp.concatenate(
+                [jnp.where(lane_q == q, piece, jnp.zeros_like(piece)) for q in range(group)], axis=0
+            ))
+        occupied = jnp.dot(
+            jnp.concatenate(columns, axis=1), amps[...], preferred_element_type=jnp.float32
+        )
+        for q in range(group):
+            partial_sum = jnp.concatenate(
+                [got[step, s, :, q * virt:(q + 1) * virt].astype(jnp.float32) for s in range(n)],
+                axis=1,
+            )
+            value = partial_sum - occupied[q * rows:(q + 1) * rows]
+            dressed[step * group + q] = value.astype(jnp.bfloat16)
+        out_copy(step).start()
+        return carry
+
+    lax.fori_loop(0, steps, consume, 0)
+
+    for copy in coulombs:
+        copy.wait()
+    coulomb = coul_sent[...]
+    for d in range(n - 1):
+        coulomb = coulomb + coul_got[d]
+    gram[0:coulomb.shape[0], 0:coulomb.shape[1]] = coulomb
+
+    fock_ref[...] = jnp.zeros_like(fock_ref)
+
+    def add_up(step, carry):
+        lines = gram[0:coulomb.shape[0], 0:coulomb.shape[1]]
+        at_row = lax.broadcasted_iota(jnp.int32, lines.shape, 0) == step
+        lane = lax.broadcasted_iota(jnp.int32, lines.shape, 1)
+        total = fock_ref[...]
+        for q in range(group):
+            weight = jnp.sum(jnp.where(at_row & (lane == q), lines, 0.0))
+            total = total + weight * dressed[step * group + q].astype(jnp.float32)
+        fock_ref[...] = total
+        return carry
+
+    lax.fori_loop(0, steps, add_up, 0)
+
+    for k, partner in enumerate(partners):
+        fock_sent[k] = fock_ref[...]
+        copy = remote(
+            fock_sent.at[k], fock_got.at[k], fock_send.at[k], fock_recv.at[k], {"pb": partner}
+        )
+        copy.start()
+        copy.wait()
+        fock_ref[...] = fock_sent[k] + fock_got[k]
+    fock_ref[...] = fock_ref[...] * (2.0 / (batch * n_pb))
+
+    def finish(step, carry):
+        out_copy(step).wait()
+        return carry
+
+    lax.fori_loop(0, steps, finish, 0)
+
+
+def fused(n, n_pb, group, chol_vv, chol_ov, chol_oo, chol_vo, amplitudes):
+    batch, virt, whole_virt = chol_vv.shape
+    rows, occ = chol_ov.shape[1], chol_oo.shape[2]
+    steps = batch // group
+    wide, deep = group * virt, group * rows
+    lines = -(-steps // 8) * 8
+    bf16, f32 = jnp.bfloat16, jnp.float32
+    dma = pltpu.SemaphoreType.DMA
+    hops = max(1, n_pb // 2)
+    whole = pl.BlockSpec(memory_space=pltpu.VMEM)
+    hbm = pl.BlockSpec(memory_space=pl.ANY)
+    return pl.pallas_call(
+        functools.partial(kernel, n, n_pb, group),
+        out_shape=(
+            jax.ShapeDtypeStruct((batch, rows, whole_virt), bf16),
+            jax.ShapeDtypeStruct((rows, whole_virt), f32),
+        ),
+        in_specs=[hbm, hbm, hbm, hbm, whole],
+        out_specs=(hbm, whole),
+        scratch_shapes=[
+            pltpu.VMEM((2, group, virt, whole_virt), bf16),
+            pltpu.VMEM((2, group, rows, whole_virt), bf16),
+            pltpu.VMEM((2, group, rows, occ), bf16),
+            pltpu.VMEM((2, group, virt, occ), bf16),
+            pltpu.VMEM((whole_virt, occ), bf16),
+            pltpu.VMEM((n * deep, whole_virt), bf16),
+            pltpu.VMEM((occ, whole_virt), f32),
+            pltpu.VMEM((rows, occ), f32),
+            pltpu.VMEM((steps, occ, wide + deep), bf16),
+            pltpu.VMEM((steps, n, rows, wide + deep), bf16),
+            pltpu.VMEM((batch, rows, whole_virt), bf16),
+            pltpu.VMEM((lines, 128), f32),
+            pltpu.VMEM((n - 1, lines, 128), f32),
+            pltpu.VMEM((hops, rows, whole_virt), f32),
+            pltpu.VMEM((hops, rows, whole_virt), f32),
+            dma((2, 4)), dma, dma((n - 1,)), dma((n - 1,)),
+            dma((steps, n - 1)), dma((steps, n - 1)),
+            dma((n - 1,)), dma((n - 1,)), dma((hops,)), dma((hops,)), dma((steps,)),
+        ],
+        compiler_params=pltpu.CompilerParams(
+            collective_id=0, has_side_effects=True, vmem_limit_bytes=60 * 1024 * 1024
+        ),
+    )(chol_vv, chol_ov, chol_oo, jnp.swapaxes(chol_vo, 1, 2), amplitudes.T)
+
+
+def group_size(batch, virt, rows):
+    for group in range(1, batch + 1):
+        if batch % group == 0 and group * virt % 128 == 0 and group * rows % 128 == 0:
+            return group
+    return None
+
+
 def solution(mesh):
+    n, n_pb = mesh.shape["pq"], mesh.shape["pb"]
     in_specs = (
         P("pb", "pq", None),
         P("pb", "pq", None),
@@ -42,6 +287,17 @@
         P(None, "pq"),
     )
     out_specs = (P("pb", "pq", None), P("pq", None))
+
+    def body(chol_vv, chol_ov, chol_oo, chol_vo, amplitudes):
+        batch, virt, unused = chol_vv.shape
+        rows, occ = chol_ov.shape[1], chol_oo.shape[2]
+        group = group_size(batch, virt, rows)
+        fits = group is not None and group <= 8 and virt % 16 == 0 and rows % 16 == 0
+        fits = fits and occ % 128 == 0 and n_pb in (1, 2, 4) and n > 1 and batch // group <= rows
+        if fits:
+            return fused(n, n_pb, group, chol_vv, chol_ov, chol_oo, chol_vo, amplitudes)
+        return per_device(chol_vv, chol_ov, chol_oo, chol_vo, amplitudes)
+
     return jax.shard_map(
-        per_device, mesh=mesh, in_specs=in_specs, out_specs=out_specs, check_vma=False
+        body, mesh=mesh, in_specs=in_specs, out_specs=out_specs, check_vma=False
     )

time: 395 us -> 176 us (0.45)
  waiting for transfers between devices: 239 us -> 0 us
  Pallas kernels: 0 us -> 169 us
  blocking collectives: 54.1 us -> 0 us
  matrix products: 43.3 us -> 0 us
  local copies, waits for them, and re-layouts: 34.7 us -> 5.78 us
  between operations: 14.1 us -> 0.65 us
  starting transfers between devices: 5.01 us -> 0 us
    pallas_call x0 -> x1, Pallas kernels: none -> 169 us  [fused(): pl.pallas_call(functools.partial(kernel, n, n_pb, group), out_shape=(jax....]
    all_to_all x1 -> x0, waiting for transfers between devices: 136 us -> none  [per_device(): lax.all_to_all(local_dressed, 'pq', split_axis=1, concat_axis=2, tiled=True)]
    all_gather x1 -> x0, waiting for transfers between devices: 73.5 us -> none  [per_device(): lax.all_gather(lprime, 'pq', axis=1, tiled=True)]
    dot_general x4 -> x0, matrix products: 43.3 us -> none  [the longest x1 19.8 us: per_device(): jnp.einsum('qab,ib->qia', chol_vv, whole_amps, preferred_element_type=jnp...]
    all_gather x1 -> x0, blocking collectives: 34.5 us -> none  [per_device(): whole_amps = lax.all_gather(amplitudes, 'pq', axis=1, tiled=True)]
    psum x1 -> x0, waiting for transfers between devices: 29.6 us -> none  [per_device(): fock_ov = lax.psum(local_fock, 'pb') / (batch * lax.axis_size('pb'))]
    all_to_all x3 -> x0, local copies, waits for them, and re-layouts: 24.4 us -> none  [per_device(): lax.all_to_all(local_dressed, 'pq', split_axis=1, concat_axis=2, tiled=True)]
    psum x1 -> x0, blocking collectives: 19.7 us -> none  [per_device(): coulomb = lax.psum(local_coulomb, 'pq')]
  transfers between devices with their start and end apart: 3 -> 0, of which waited for: 3 -> 0; matrix products, arithmetic and copies ran while one was open for 5% -> 0% of each run, Pallas kernels for 0% -> 0%
where the time goes in v1:
time: 176 us; the launch traced here: 175 us
  Pallas kernels  169 us (96%)
  local copies, waits for them, and re-layouts  5.78 us (3%)
    pallas_call x1, Pallas kernels, fused(): pl.pallas_call(functools.partial(kernel, n, n_pb, group), out_shape=(jax....  169 us
    unnamed x4, local copies, waits for them, and re-layouts  5.78 us

profile of v1, /device:TPU:0, one launch (start us, length us, event | category | flops | bytes accessed | tf_op | source)
XLA Modules:
  0.0 175.4 jit_solution(11285397615762443747)
XLA Ops:
  0.6 169.0 %shard_map.68 = (bf16[44,32,1792]{2,1,0:T(8,128)(2,1)}, f32[32,1792]{1,0:T(8,128)}) custom-call(bf16[44,224,1792]{2,1,0:T(8,128)(2,1)} %vv_hbm.1, bf16[44,32,1792]{2,1,0:T(8,128)(2,1)} %ov_hbm.1, bf16[44,32,256]{2,1,0:T(8,128)(2,1)} %oo_hbm.1, bf16[44,224,256]{2,1,0:T(8,128)(2,1)} %bitcast.2, bf16[224,256]{1,0:T(8,128)(2,1)} %bitcast.3), custom_call_target="tpu_custom_call" | custom-call | tf_op jit(solution)/shard_map/pallas_call | solution.py:239
  169.6 0.0 copy-start
  169.6 5.1 %copy.9 = bf16[44,32,1792]{2,1,0:T(8,128)(2,1)} copy(bf16[44,32,1792]{2,1,0:T(8,128)(2,1)} %get-tuple-element.4) | data formatting | bytes 10092544
  174.7 0.0 copy-done
  174.7 0.7 copy.10
Async XLA Ops:
  169.6 5.1 %copy-start = (f32[32,1792]{1,0:T(8,128)S(1)}, f32[32,1792]{1,0:T(8,128)}, u32[]{:S(2)}) copy-start(f32[32,1792]{1,0:T(8,128)} %get-tuple-element.5) | copy-start | bytes 688132

commit v2 on v1

--- a/solution.py
+++ b/solution.py
@@ -42,11 +42,11 @@
 def kernel(
     n, n_pb, group,
     vv_hbm, ov_hbm, oo_hbm, vo_hbm, amps_ref,
-    out_hbm, fock_ref,
+    dressed, fock_ref,
     vv_buf, ov_buf, oo_buf, vo_buf, amps_t, amps, tiled, gram,
-    sent, got, dressed, coul_sent, coul_got, fock_sent, fock_got,
+    sent, got, coul_sent, coul_got, fock_sent, fock_got,
     load_sem, own_sem, gather_send, gather_recv, send_sem, recv_sem,
-    coul_send, coul_recv, fock_send, fock_recv, out_sem,
+    coul_send, coul_recv, fock_send, fock_recv,
 ):
     me = lax.axis_index("pq")
     mine = lax.axis_index("pb")
@@ -55,9 +55,9 @@
     steps = batch // group
     wide, deep = group * virt, group * rows
     peers = [lax.rem(me + d, n) for d in range(1, n)]
-    partners = [mine + 1 - 2 * lax.rem(mine, 2)] if n_pb >= 2 else []
-    if n_pb >= 4:
-        partners.append(lax.rem(mine + 2, 4))
+    core, place = lax.rem(mine, 2), mine // 2
+    mate, across = mine + 1 - 2 * core, lax.rem(mine + 2, 4)
+    partners = [mate, across]
 
     def loads(step, slot):
         part = pl.ds(step * group, group)
@@ -83,18 +83,44 @@
             device_id=where, device_id_type=MESH,
         )
 
-    own_block = pl.ds(pl.multiple_of(me * virt, 16), virt)
+    half_virt, half_occ = virt // 2, occ // 2
+    own_columns = pl.ds(pl.multiple_of(core * half_occ, 128), half_occ)
+
+    def quarter(owner):
+        first = pl.multiple_of(owner * virt + place * half_virt, 16)
+        return amps_t.at[pl.ds(first, half_virt), own_columns]
+
+    own_quarter = amps_ref.at[pl.ds(pl.multiple_of(place * half_virt, 16), half_virt), own_columns]
     gathers = [
-        remote(amps_ref, amps_t.at[own_block], gather_send.at[d], gather_recv.at[d], {"pq": peer})
+        remote(own_quarter, quarter(me), gather_send.at[0, d], gather_recv.at[0, d], {"pq": peer})
         for d, peer in enumerate(peers)
     ]
     for copy in gathers:
         copy.start()
+    own_block = pl.ds(pl.multiple_of(me * virt, 16), virt)
     own = pltpu.make_async_copy(amps_ref, amps_t.at[own_block], own_sem)
     own.start()
     own.wait()
-    for copy in gathers:
-        copy.wait()
+    owners = [lax.rem(me + n - 1 - d, n) for d in range(n - 1)]
+    crossing = [
+        remote(quarter(owner), quarter(owner), gather_send.at[1, d], gather_recv.at[1, d], {"pb": across})
+        for d, owner in enumerate(owners)
+    ]
+    swaps = []
+    for d, owner in enumerate(owners):
+        block = pl.ds(pl.multiple_of(owner * virt, 16), virt)
+        half = amps_t.at[block, own_columns]
+        swaps.append(remote(half, half, gather_send.at[2, d], gather_recv.at[2, d], {"pb": mate}))
+    for d in range(n - 1):
+        gathers[d].wait_recv()
+        crossing[d].start()
+    for d in range(n - 1):
+        crossing[d].wait_recv()
+        swaps[d].start()
+    for d in range(n - 1):
+        swaps[d].wait_recv()
+    for copy in gathers + crossing + swaps:
+        copy.wait_send()
 
     for s in range(n):
         block = amps_t[s * virt:(s + 1) * virt, :]
@@ -114,6 +140,8 @@
             got.at[step, me],
             send_sem.at[step, d], recv_sem.at[step, d], {"pq": peers[d]},
         )
+
+    early = min(steps, 5)
 
     def produce(step, carry):
         slot = lax.rem(step, 2)
@@ -144,8 +172,12 @@
             held = jnp.where(at_row & (lane == q), value, held)
         coul_sent[...] = held
         got[step, me] = sent[step, pl.ds(pl.multiple_of(me * rows, 16), rows), :]
-        for d in range(n - 1):
-            exchange(step, d).start()
+
+        @pl.when(step < early)
+        def _():
+            for d in range(n - 1):
+                exchange(step, d).start()
+
         return carry
 
     lax.fori_loop(0, steps, produce, 0)
@@ -157,9 +189,20 @@
     for copy in coulombs:
         copy.start()
 
-    def out_copy(step):
-        part = pl.ds(step * group, group)
-        return pltpu.make_async_copy(dressed.at[part], out_hbm.at[part], out_sem.at[step])
+    def send(step, carry):
+        for d in range(n - 1):
+            exchange(step, d).start()
+        return carry
+
+    lax.fori_loop(early, steps, send, 0)
+
+    for copy in coulombs:
+        copy.wait()
+    coulomb = coul_sent[...]
+    for d in range(n - 1):
+        coulomb = coulomb + coul_got[d]
+    coul_sent[...] = coulomb
+    fock_ref[...] = jnp.zeros_like(fock_ref)
 
     def consume(step, carry):
         for d in range(n - 1):
@@ -174,55 +217,41 @@
         occupied = jnp.dot(
             jnp.concatenate(columns, axis=1), amps[...], preferred_element_type=jnp.float32
         )
+        weights = coul_sent[...]
+        at_row = lax.broadcasted_iota(jnp.int32, weights.shape, 0) == step
+        lane = lax.broadcasted_iota(jnp.int32, weights.shape, 1)
+        total = fock_ref[...]
         for q in range(group):
             partial_sum = jnp.concatenate(
                 [got[step, s, :, q * virt:(q + 1) * virt].astype(jnp.float32) for s in range(n)],
                 axis=1,
             )
-            value = partial_sum - occupied[q * rows:(q + 1) * rows]
-            dressed[step * group + q] = value.astype(jnp.bfloat16)
-        out_copy(step).start()
-        return carry
-
-    lax.fori_loop(0, steps, consume, 0)
-
-    for copy in coulombs:
-        copy.wait()
-    coulomb = coul_sent[...]
-    for d in range(n - 1):
-        coulomb = coulomb + coul_got[d]
-    gram[0:coulomb.shape[0], 0:coulomb.shape[1]] = coulomb
-
-    fock_ref[...] = jnp.zeros_like(fock_ref)
-
-    def add_up(step, carry):
-        lines = gram[0:coulomb.shape[0], 0:coulomb.shape[1]]
-        at_row = lax.broadcasted_iota(jnp.int32, lines.shape, 0) == step
-        lane = lax.broadcasted_iota(jnp.int32, lines.shape, 1)
-        total = fock_ref[...]
-        for q in range(group):
-            weight = jnp.sum(jnp.where(at_row & (lane == q), lines, 0.0))
-            total = total + weight * dressed[step * group + q].astype(jnp.float32)
+            value = (partial_sum - occupied[q * rows:(q + 1) * rows]).astype(jnp.bfloat16)
+            dressed[step * group + q] = value
+            weight = jnp.sum(jnp.where(at_row & (lane == q), weights, 0.0))
+            total = total + weight * value.astype(jnp.float32)
         fock_ref[...] = total
         return carry
 
-    lax.fori_loop(0, steps, add_up, 0)
-
-    for k, partner in enumerate(partners):
-        fock_sent[k] = fock_ref[...]
+    lax.fori_loop(0, steps, consume, 0)
+
+    half_rows = rows // 2
+    own_half = pl.ds(pl.multiple_of(core * half_rows, 8), half_rows)
+    mate_half = pl.ds(pl.multiple_of((1 - core) * half_rows, 8), half_rows)
+
+    def swap(k, value, partner):
+        fock_sent[k] = value
         copy = remote(
             fock_sent.at[k], fock_got.at[k], fock_send.at[k], fock_recv.at[k], {"pb": partner}
         )
         copy.start()
         copy.wait()
-        fock_ref[...] = fock_sent[k] + fock_got[k]
-    fock_ref[...] = fock_ref[...] * (2.0 / (batch * n_pb))
-
-    def finish(step, carry):
-        out_copy(step).wait()
-        return carry
-
-    lax.fori_loop(0, steps, finish, 0)
+        return fock_got[k]
+
+    both = swap(0, fock_ref[mate_half, :], mate) + fock_ref[own_half, :]
+    every = (swap(1, both, across) + both) * (2.0 / (batch * n_pb))
+    fock_ref[own_half, :] = every
+    fock_ref[mate_half, :] = swap(2, every, mate)
 
 
 def fused(n, n_pb, group, chol_vv, chol_ov, chol_oo, chol_vo, amplitudes):
@@ -233,17 +262,17 @@
     lines = -(-steps // 8) * 8
     bf16, f32 = jnp.bfloat16, jnp.float32
     dma = pltpu.SemaphoreType.DMA
-    hops = max(1, n_pb // 2)
+    hops = 3
     whole = pl.BlockSpec(memory_space=pltpu.VMEM)
     hbm = pl.BlockSpec(memory_space=pl.ANY)
     return pl.pallas_call(
         functools.partial(kernel, n, n_pb, group),
         out_shape=(
-            jax.ShapeDtypeStruct((batch, rows, whole_virt), bf16),
+            pltpu.VMEM((batch, rows, whole_virt), bf16),
             jax.ShapeDtypeStruct((rows, whole_virt), f32),
         ),
         in_specs=[hbm, hbm, hbm, hbm, whole],
-        out_specs=(hbm, whole),
+        out_specs=(whole, whole),
         scratch_shapes=[
             pltpu.VMEM((2, group, virt, whole_virt), bf16),
             pltpu.VMEM((2, group, rows, whole_virt), bf16),
@@ -255,17 +284,16 @@
             pltpu.VMEM((rows, occ), f32),
             pltpu.VMEM((steps, occ, wide + deep), bf16),
             pltpu.VMEM((steps, n, rows, wide + deep), bf16),
-            pltpu.VMEM((batch, rows, whole_virt), bf16),
             pltpu.VMEM((lines, 128), f32),
             pltpu.VMEM((n - 1, lines, 128), f32),
-            pltpu.VMEM((hops, rows, whole_virt), f32),
-            pltpu.VMEM((hops, rows, whole_virt), f32),
-            dma((2, 4)), dma, dma((n - 1,)), dma((n - 1,)),
+            pltpu.VMEM((hops, rows // 2, whole_virt), f32),
+            pltpu.VMEM((hops, rows // 2, whole_virt), f32),
+            dma((2, 4)), dma, dma((3, n - 1)), dma((3, n - 1)),
             dma((steps, n - 1)), dma((steps, n - 1)),
-            dma((n - 1,)), dma((n - 1,)), dma((hops,)), dma((hops,)), dma((steps,)),
+            dma((n - 1,)), dma((n - 1,)), dma((hops,)), dma((hops,)),
         ],
         compiler_params=pltpu.CompilerParams(
-            collective_id=0, has_side_effects=True, vmem_limit_bytes=60 * 1024 * 1024
+            collective_id=0, has_side_effects=True, vmem_limit_bytes=44 * 1024 * 1024
         ),
     )(chol_vv, chol_ov, chol_oo, jnp.swapaxes(chol_vo, 1, 2), amplitudes.T)
 
@@ -292,8 +320,8 @@
         batch, virt, unused = chol_vv.shape
         rows, occ = chol_ov.shape[1], chol_oo.shape[2]
         group = group_size(batch, virt, rows)
-        fits = group is not None and group <= 8 and virt % 16 == 0 and rows % 16 == 0
-        fits = fits and occ % 128 == 0 and n_pb in (1, 2, 4) and n > 1 and batch // group <= rows
+        fits = group is not None and group <= 8 and virt % 32 == 0 and rows % 16 == 0
+        fits = fits and occ % 256 == 0 and n_pb == 4 and n > 1 and batch // group <= rows
         if fits:
             return fused(n, n_pb, group, chol_vv, chol_ov, chol_oo, chol_vo, amplitudes)
         return per_device(chol_vv, chol_ov, chol_oo, chol_vo, amplitudes)

time: 176 us -> 159 us (0.903)
  Pallas kernels: 169 us -> 152 us
    pallas_call x1, Pallas kernels: 169 us -> 152 us  [fused(): pl.pallas_call(functools.partial(kernel, n, n_pb, group), out_shape=(pltp...]
    unnamed x4 -> x6, local copies, waits for them, and re-layouts: 5.78 us -> 4.98 us
where the time goes in v2:
time: 159 us; the launch traced here: 158 us
  Pallas kernels  152 us (96%)
  local copies, waits for them, and re-layouts  4.98 us (3%)
    pallas_call x1, Pallas kernels, fused(): pl.pallas_call(functools.partial(kernel, n, n_pb, group), out_shape=(pltp...  152 us
    unnamed x6, local copies, waits for them, and re-layouts  4.98 us

profile of v2, /device:TPU:0, one launch (start us, length us, event | category | flops | bytes accessed | tf_op | source)
XLA Modules:
  0.0 157.8 jit_solution(4424747369512275627)
XLA Ops:
  0.6 0.0 copy-start
  0.6 1.1 copy-done
  1.7 0.0 copy-start.1
  1.7 0.9 copy-done.1
  2.6 152.2 %shard_map.68 = (bf16[44,32,1792]{2,1,0:T(8,128)(2,1)S(1)}, f32[32,1792]{1,0:T(8,128)S(1)}) custom-call(bf16[44,224,1792]{2,1,0:T(8,128)(2,1)} %vv_hbm.1, bf16[44,32,1792]{2,1,0:T(8,128)(2,1)} %ov_hbm.1, bf16[44,32,256]{2,1,0:T(8,128)(2,1)S(1)} %copy-done, bf16[44,224,256]{2,1,0:T(8,128)(2,1)} %bitcast.3, bf16[224,256]{1,0:T(8,128)(2,1)S(1)} %bitcast.2), custom_call_target="tpu_custom_call" | custom-call | tf_op jit(solution)/shard_map/pallas_call | solution.py:268
  154.9 2.3 %copy.9 = bf16[44,32,1792]{2,1,0:T(8,128)(2,1)} copy(bf16[44,32,1792]{2,1,0:T(8,128)(2,1)S(1)} %get-tuple-element.2) | data formatting | bytes 10092544
  157.2 0.7 copy.10
Async XLA Ops:
  0.6 1.1 copy-start
  1.7 0.9 copy-start.1
